TPU v7x, 512 devices: a whole 4x8x8 slice. The times are simulated.
512 devices in a mesh: dp: 8 (over y_hi, core), expert: 64 (over y_lo, x, z).
Axes of the slice: x: 4, y: 8 (y_hi: 4, y_lo: 2; y = y_hi * 2 + y_lo), z: 8, core: 2. Of those that a mesh axis runs over, the one named last changes fastest.
Arguments:
- weights: bfloat16 [16, 3584, 512], P(None, ('dp', 'expert')), may hold values from -0.09375 to 0.09375
- first_moment: float32 [16, 3584, 512], P(None, ('dp', 'expert')), may hold values from -3 to 3
- second_moment: float32 [16, 3584, 512], P(None, ('dp', 'expert')), may hold values from 0.05 to 2
- placement: int32 [64], replicated, may hold values from 0 to 15, as said below
- block_counts: int32 [8, 64], P('dp', 'expert'), may hold values from 1 to 2
- tokens: bfloat16 [8, 64, 256, 3584], P('dp', 'expert'), may hold values from -6 to 6
- hidden_grad: bfloat16 [8, 64, 256, 256], P('dp', 'expert'), may hold values from -1.1953125 to 1.1953125
Outputs:
- new_weights: bfloat16 [64, 3584, 512], P('expert', 'dp')
- new_first: float32 [64, 3584, 512], P('expert', 'dp')
- new_second: float32 [64, 3584, 512], P('expert', 'dp')
Inputs may be any that keep to these rules, and one draw needn't show every extreme that they name: `placement`: every expert block 0 to 15 is owned by at least one device. `block_counts`: the rows after a device's live blocks are padding.
All inputs are finite; a program needn't handle non-finite values.
Results may differ from a plain program's by a relative error of at most 0.015.
Values may be sent and summed in bfloat16 or wider, within the bound.
No kernel may reach another device: no remote copies, remote signals or barrier semaphores. Data moves between devices by JAX's collectives and lax.ppermute only.
A program may use at most 64 MiB of HBM per device.

v0:
```python
import jax
import jax.numpy as jnp
from jax import lax
from jax.sharding import PartitionSpec as P

BLOCK = 128


beta_first = 0.9
beta_second = 0.95
learning_rate = 0.001
weight_decay = 0.1
adam_epsilon = 1e-08
adam_steps = 10.0


def silu_grads(projected, upstream, live_mask):
    half_width = projected.shape[1] // 2
    gate_part = projected[:, :half_width]
    upward = projected[:, half_width:]
    sigmoid_gate = jax.nn.sigmoid(gate_part)
    masked = jnp.where(live_mask, upstream.astype(jnp.float32), 0.0)
    grad_gate = masked * upward * sigmoid_gate * (1.0 + gate_part * (1.0 - sigmoid_gate))
    grad_upward = masked * gate_part * sigmoid_gate
    return jnp.concatenate([grad_gate, grad_upward], axis=1).astype(jnp.bfloat16)


def adam_update(params, first_moment, second_moment, gradient):
    moment_one = beta_first * first_moment + (1.0 - beta_first) * gradient
    moment_two = beta_second * second_moment + (1.0 - beta_second) * gradient * gradient
    correct_one = 1.0 - beta_first**adam_steps
    correct_two = 1.0 - beta_second**adam_steps
    params_full = params.astype(jnp.float32)
    step_size = (
        moment_one / correct_one / (jnp.sqrt(moment_two / correct_two) + adam_epsilon)
        + weight_decay * params_full
    )
    return ((params_full - learning_rate * step_size).astype(jnp.bfloat16), moment_one, moment_two)


def on_device(weights, first_moment, second_moment, placement, block_counts, tokens, hidden_grad):
    expert_count = lax.axis_size("expert")
    block_total = weights.shape[0]
    span_rows = weights.shape[1]
    col_total = weights.shape[2]
    inputs = tokens[0, 0]
    row_total = inputs.shape[0]
    owner_table = (placement[:, None] == jnp.arange(block_total)[None, :]).astype(jnp.float32)
    live_mask = (jnp.arange(row_total) < BLOCK * block_counts[0, 0])[:, None]
    outgoing = jnp.take(weights, placement, axis=0)
    arrived = lax.all_to_all(outgoing, "expert", split_axis=0, concat_axis=0, tiled=True)
    own_rows = arrived.reshape(expert_count * span_rows, col_total)
    columns = inputs
    projected = jnp.dot(
        columns,
        lax.all_gather(own_rows, "dp", axis=0, tiled=True),
        preferred_element_type=jnp.float32,
    )
    grad_proj = silu_grads(projected, hidden_grad[0, 0], live_mask)
    columns = inputs
    summed_data = lax.psum_scatter(
        lax.dot_general(
            columns, grad_proj, (((0,), (0,)), ((), ())), preferred_element_type=jnp.float32
        ).astype(jnp.bfloat16),
        "dp",
        scatter_dimension=0,
        tiled=True,
    ).astype(jnp.float32)
    at_home = lax.all_to_all(
        summed_data.reshape(expert_count, span_rows, col_total),
        "expert",
        split_axis=0,
        concat_axis=0,
        tiled=True,
    )
    block_grad = lax.dot_general(
        owner_table,
        at_home.reshape(expert_count, span_rows * col_total),
        (((0,), (0,)), ((), ())),
        precision=lax.Precision.HIGHEST,
    )
    block_grad = block_grad.reshape(block_total, span_rows, col_total)
    first_sent = jnp.take(first_moment, placement, axis=0)
    second_sent = jnp.take(second_moment, placement, axis=0)
    grad_sent = jnp.take(block_grad, placement, axis=0)
    first_here, second_here, grad_here = (
        lax.all_to_all(first_sent, "expert", split_axis=0, concat_axis=0, tiled=True),
        lax.all_to_all(second_sent, "expert", split_axis=0, concat_axis=0, tiled=True),
        lax.all_to_all(grad_sent, "expert", split_axis=0, concat_axis=0, tiled=True),
    )
    own_shape = (expert_count * span_rows, col_total)
    updated, moment_one, moment_two = adam_update(
        own_rows,
        first_here.reshape(own_shape),
        second_here.reshape(own_shape),
        grad_here.reshape(own_shape),
    )
    return (updated[None], moment_one[None], moment_two[None])


def solution(mesh):
    in_specs = (
        P(None, ("dp", "expert"), None),
        P(None, ("dp", "expert"), None),
        P(None, ("dp", "expert"), None),
        P(),
        P("dp", "expert"),
        P("dp", "expert", None, None),
        P("dp", "expert", None, None),
    )
    out_specs = (P("expert", "dp", None), P("expert", "dp", None), P("expert", "dp", None))
    return jax.shard_map(
        on_device, mesh=mesh, in_specs=in_specs, out_specs=out_specs, check_vma=False
    )
```

profile of v0, /device:TPU:16, one launch (start us, length us, event | category | flops | bytes accessed | tf_op | source)
XLA Modules:
  0.0 295.5 jit_solution(6079910095113931859)
XLA Ops:
  7.2 0.0 copy-start
  7.2 0.0 all-gather.2.cloned.1.call-start
  7.2 0.8 compare_select_fusion
  8.0 0.7 compare_and_fusion
  8.7 0.0 copy-start.5
  8.7 2.9 gather_fusion
  11.6 0.1 broadcast_select_fusion.3
  11.7 0.3 copy.29
  12.0 33.6 %all_to_all.25 = bf16[64,7,512]{2,1,0:T(8,128)(2,1)S(1)} all-to-all(bf16[64,7,512]{2,1,0:T(8,128)(2,1)S(1)} %copy.29), channel_id=1, replica_groups=mesh['dp'=8,'expert'=64] {'expert'}, dimensions={0} | all-to-all | bytes 917504 | tf_op jit(solution)/shard_map/all_to_all | solution.py:51
  45.6 0.9 reshape.163
  46.5 0.0 all-gather.2.cloned.1.call-update
  46.5 0.0 reduce-scatter.4.cloned.1.call-start
  46.6 0.0 copy-done.5
  46.6 0.1 copy.31
  47.4 43.8 %all-gather.2.cloned.1.call-done = bf16[3584,512]{1,0:T(8,128)(2,1)} async-done(((bf16[448,512]{1,0:T(8,128)(2,1)}), bf16[3584,512]{1,0:T(8,128)(2,1)}) %all-gather.2.cloned.1.call-update) | async-done | bytes 3670032 | tf_op jit(solution)/shard_map/all_gather | solution.py:56
  91.2 3.2 %fusion.4 = f32[256,512]{0,1:T(8,128)S(1)} fusion(bf16[3584,512]{1,0:T(8,128)(2,1)} %all-gather.2.cloned.1.call-done, bf16[1,1,256,3584]{3,2,1,0:T(8,128)(2,1)S(1)} %copy-done), kind=kOutput, calls=%fused_computation.10 | convolution fusion | flops 939524096 | bytes 6029312 | tf_op jit(solution)/shard_map/dot_general | solution.py:54
  94.4 0.2 fusion.13
  94.5 3.0 %fusion = bf16[3584,512]{0,1:T(8,128)(2,1)} fusion(bf16[1,1,256,3584]{3,2,1,0:T(8,128)(2,1)S(1)} %copy-done, bf16[256,256]{0,1:T(8,128)(2,1)S(1)} %get-tuple-element.8, bf16[256,256]{0,1:T(8,128)(2,1)S(1)} %get-tuple-element.7), kind=kOutput, calls=%fused_computation.5 | convolution fusion | flops 941883392 | bytes 5767168 | tf_op jit(solution)/shard_map/dot_general | solution.py:62
  97.5 5.9 %copy.36 = bf16[3584,512]{1,0:T(8,128)(2,1)} copy(bf16[3584,512]{0,1:T(8,128)(2,1)} %fusion) | data formatting | bytes 7340032
  103.4 0.0 reduce-scatter.4.cloned.1.call-update
  103.4 0.9 copy-done.1
  104.4 2.8 gather_fusion.1
  107.1 2.8 gather_fusion.3
  109.9 2.6 broadcast_select_fusion.1
  112.6 1.5 copy.30
  114.1 10.8 %all-to-all-start.1 = ((f32[64,7,512]{2,1,0:T(8,128)}), f32[64,7,512]{2,1,0:T(8,128)S(1)}, u32[]{:S(2)}, u32[]{:S(2)}) async-start(f32[64,7,512]{2,1,0:T(8,128)} %copy.30), calls=%async_computation.1 | async-start | bytes 2097152 | tf_op jit(solution)/shard_map/all_to_all | solution.py:87
  124.9 0.0 copy-start.6
  124.9 40.7 %reduce-scatter.4.cloned.1.call-done = bf16[448,512]{1,0:T(8,128)(2,1)} async-done(((bf16[3584,512]{1,0:T(8,128)(2,1)}), bf16[448,512]{1,0:T(8,128)(2,1)}) %reduce-scatter.4.cloned.1.call-update) | async-done | bytes 458768 | tf_op jit(solution)/shard_map/reduce_scatter | solution.py:61
  165.6 2.1 reshape.171
  167.7 0.0 all-to-all-done.1
  167.7 13.7 %all-to-all-start.2 = ((f32[64,7,512]{2,1,0:T(8,128)}), f32[64,7,512]{2,1,0:T(8,128)}, u32[]{:S(2)}, u32[]{:S(2)}) async-start(f32[64,7,512]{2,1,0:T(8,128)} %reshape.171), calls=%async_computation.2 | async-start | bytes 2097152 | tf_op jit(solution)/shard_map/all_to_all | solution.py:69
  181.4 2.7 copy.35
  184.1 26.4 %all-to-all-done.2 = f32[64,7,512]{2,1,0:T(8,128)} async-done(((f32[64,7,512]{2,1,0:T(8,128)}), f32[64,7,512]{2,1,0:T(8,128)}, u32[]{:S(2)}, u32[]{:S(2)}) %all-to-all-start.2) | async-done | bytes 917536 | tf_op jit(solution)/shard_map/all_to_all | solution.py:69
  210.5 7.0 %all-to-all-start.4 = ((f32[64,7,512]{2,1,0:T(8,128)}), f32[64,7,512]{2,1,0:T(8,128)}, u32[]{:S(2)}, u32[]{:S(2)}) async-start(f32[64,7,512]{2,1,0:T(8,128)} %copy.35), calls=%async_computation.4 | async-start | bytes 2097152 | tf_op jit(solution)/shard_map/all_to_all | solution.py:88
  217.6 2.1 fusion.8
  219.7 0.1 copy.34
  219.8 1.6 gather_fusion.2
  221.5 2.5 broadcast_select_fusion
  223.9 24.3 %all-to-all-done.4 = f32[64,7,512]{2,1,0:T(8,128)} async-done(((f32[64,7,512]{2,1,0:T(8,128)}), f32[64,7,512]{2,1,0:T(8,128)}, u32[]{:S(2)}, u32[]{:S(2)}) %all-to-all-start.4) | async-done | bytes 917536 | tf_op jit(solution)/shard_map/all_to_all | solution.py:88
  248.2 5.5 %all-to-all-start.3 = ((f32[64,7,512]{2,1,0:T(8,128)}), f32[64,7,512]{2,1,0:T(8,128)}, u32[]{:S(2)}, u32[]{:S(2)}) async-start(f32[64,7,512]{2,1,0:T(8,128)} %broadcast_select_fusion), calls=%async_computation.3 | async-start | bytes 2097152 | tf_op jit(solution)/shard_map/all_to_all | solution.py:89
  253.7 1.1 reshape.168
  254.8 1.1 broadcast_multiply_fusion.1
  255.9 2.3 mul.128
  258.2 1.4 broadcast_multiply_fusion
  259.6 1.1 mul.138
  260.6 23.0 %all-to-all-done.3 = f32[64,7,512]{2,1,0:T(8,128)} async-done(((f32[64,7,512]{2,1,0:T(8,128)}), f32[64,7,512]{2,1,0:T(8,128)}, u32[]{:S(2)}, u32[]{:S(2)}) %all-to-all-start.3) | async-done | bytes 917536 | tf_op jit(solution)/shard_map/all_to_all | solution.py:89
  283.7 1.4 reshape.167
  285.0 3.6 %subtract_convert_fusion = (bf16[1,448,512]{2,1,0:T(8,128)(2,1)}, f32[1,448,512]{2,1,0:T(8,128)}, f32[1,448,512]{2,1,0:T(8,128)}) fusion(f32[1,448,512]{2,1,0:T(8,128)} %reshape.168, f32[1,448,512]{2,1,0:T(8,128)} %mul.128, f32[1,448,512]{2,1,0:T(8,128)S(1)} %reshape.167, f32[1,448,512]{2,1,0:T(8,128)} %mul.138), kind=kLoop, calls=%fused_computation.15 | loop fusion | flops 3211264 | bytes 5963776 | tf_op jit(solution)/shard_map/convert_element_type | solution.py:38
  (11 shorter events, 0.0 us)
Async XLA Ops:
  7.2 84.0 %copy-start = (bf16[1,1,256,3584]{3,2,1,0:T(8,128)(2,1)S(1)}, bf16[1,1,256,3584]{3,2,1,0:T(8,128)(2,1)}, u32[]{:S(2)}) copy-start(bf16[1,1,256,3584]{3,2,1,0:T(8,128)(2,1)} %param.14) | copy-start | bytes 5505028
  7.2 84.0 %all-gather.2.cloned.1.call-start = ((), (), s32[]{:S(2)}) async-start(), calls=%async_computation.6 | async-start | bytes 4128768 | tf_op jit(solution)/shard_map/all_gather | solution.py:56
  8.7 37.9 %copy-start.5 = (bf16[1,1,256,256]{3,2,1,0:T(8,128)(2,1)S(1)}, bf16[1,1,256,256]{3,2,1,0:T(8,128)(2,1)}, u32[]{:S(2)}) copy-start(bf16[1,1,256,256]{3,2,1,0:T(8,128)(2,1)} %param.15) | copy-start | bytes 393220
  46.5 119.0 %reduce-scatter.4.cloned.1.call-start = ((), (), s32[]{:S(2)}) async-start(), calls=%async_computation.7 | async-start | bytes 4128768 | tf_op jit(solution)/shard_map/reduce_scatter | solution.py:61
  103.4 0.9 copy-start.1
  104.4 2.8 copy-start.2
  114.1 53.6 %all-to-all-start.1 = ((f32[64,7,512]{2,1,0:T(8,128)}), f32[64,7,512]{2,1,0:T(8,128)S(1)}, u32[]{:S(2)}, u32[]{:S(2)}) async-start(f32[64,7,512]{2,1,0:T(8,128)} %copy.30), calls=%async_computation.1 | async-start | bytes 2097152 | tf_op jit(solution)/shard_map/all_to_all | solution.py:87
  124.9 92.7 %copy-start.6 = (s32[64]{0:T(128)S(1)}, s32[64]{0:T(128)}, u32[]{:S(2)}) copy-start(s32[64]{0:T(128)} %param.12) | copy-start | bytes 772
  167.7 49.9 %copy-start.3 = (f32[64,7,512]{2,1,0:T(8,128)}, f32[64,7,512]{2,1,0:T(8,128)S(1)}, u32[]{:S(2)}) copy-start(f32[64,7,512]{2,1,0:T(8,128)S(1)} %all-to-all-done.1) | copy-start | bytes 2752516
  167.7 42.9 %all-to-all-start.2 = ((f32[64,7,512]{2,1,0:T(8,128)}), f32[64,7,512]{2,1,0:T(8,128)}, u32[]{:S(2)}, u32[]{:S(2)}) async-start(f32[64,7,512]{2,1,0:T(8,128)} %reshape.171), calls=%async_computation.2 | async-start | bytes 2097152 | tf_op jit(solution)/shard_map/all_to_all | solution.py:69
  210.5 37.7 %all-to-all-start.4 = ((f32[64,7,512]{2,1,0:T(8,128)}), f32[64,7,512]{2,1,0:T(8,128)}, u32[]{:S(2)}, u32[]{:S(2)}) async-start(f32[64,7,512]{2,1,0:T(8,128)} %copy.35), calls=%async_computation.4 | async-start | bytes 2097152 | tf_op jit(solution)/shard_map/all_to_all | solution.py:88
  221.4 33.3 %copy-start.4 = (f32[64,7,512]{2,1,0:T(8,128)S(1)}, f32[64,7,512]{2,1,0:T(8,128)}, u32[]{:S(2)}) copy-start(f32[64,7,512]{2,1,0:T(8,128)} %copy-done.3) | copy-start | bytes 2752516
  248.2 35.4 %all-to-all-start.3 = ((f32[64,7,512]{2,1,0:T(8,128)}), f32[64,7,512]{2,1,0:T(8,128)}, u32[]{:S(2)}, u32[]{:S(2)}) async-start(f32[64,7,512]{2,1,0:T(8,128)} %broadcast_select_fusion), calls=%async_computation.3 | async-start | bytes 2097152 | tf_op jit(solution)/shard_map/all_to_all | solution.py:89
Sparse Core Ops, SparseCore 0:
  46.6 44.4 all-gather.1
  103.6 61.9 reduce-scatter.3
where the time goes:
time: 297 us; the launch traced here: 295 us
  waiting for transfers between devices  158 us (53%)
  starting transfers between devices  37.1 us (12%)
  blocking collectives  33.6 us (11%)
  local copies, waits for them, and re-layouts  30.4 us (10%)
  between operations  14.9 us (5%)
  other arithmetic  12.9 us (4%)
  matrix products  8.26 us (3%)
    all_gather x1, waiting for transfers between devices, on_device(): lax.all_gather(own_rows, 'dp', axis=0, tiled=True)  43.8 us
    reduce_scatter x1, waiting for transfers between devices, on_device(): lax.psum_scatter(lax.dot_general(columns, grad_proj, (((0,), (0,)), ((),...  40.7 us
    all_to_all x1, blocking collectives, on_device(): lax.all_to_all(outgoing, 'expert', split_axis=0, concat_axis=0, tiled=True)  33.6 us
    all_to_all x1, waiting for transfers between devices, on_device(): lax.all_to_all(summed_data.reshape(expert_count, span_rows, col_total), '...  26.4 us
    all_to_all x1, waiting for transfers between devices, on_device(): lax.all_to_all(second_sent, 'expert', split_axis=0, concat_axis=0, tiled=...  24.3 us
    all_to_all x1, waiting for transfers between devices, on_device(): lax.all_to_all(grad_sent, 'expert', split_axis=0, concat_axis=0, tiled=True)  23 us
    all_to_all x1, starting transfers between devices, on_device(): lax.all_to_all(summed_data.reshape(expert_count, span_rows, col_total), '...  13.7 us
    all_to_all x1, starting transfers between devices, on_device(): lax.all_to_all(first_sent, 'expert', split_axis=0, concat_axis=0, tiled=T...  10.8 us
  transfers between devices with their start and end apart: 6, of which 5 were waited for; matrix products, arithmetic and copies ran while one was open for 9% of the time, Pallas kernels for 0%

commit v1 on v0

--- a/solution.py
+++ b/solution.py
@@ -45,55 +45,39 @@
     col_total = weights.shape[2]
     inputs = tokens[0, 0]
     row_total = inputs.shape[0]
-    owner_table = (placement[:, None] == jnp.arange(block_total)[None, :]).astype(jnp.float32)
+    narrow = jnp.bfloat16
     live_mask = (jnp.arange(row_total) < BLOCK * block_counts[0, 0])[:, None]
-    outgoing = jnp.take(weights, placement, axis=0)
-    arrived = lax.all_to_all(outgoing, "expert", split_axis=0, concat_axis=0, tiled=True)
-    own_rows = arrived.reshape(expert_count * span_rows, col_total)
-    columns = inputs
-    projected = jnp.dot(
-        columns,
-        lax.all_gather(own_rows, "dp", axis=0, tiled=True),
-        preferred_element_type=jnp.float32,
-    )
+    own_shape = (expert_count * span_rows, col_total)
+    pick = (placement[:, None] == jnp.arange(block_total)[None, :]).astype(narrow)
+    same = (placement[:, None] == placement[None, :]).astype(narrow)
+
+    def exchange(values):
+        return lax.all_to_all(values, "expert", split_axis=0, concat_axis=0, tiled=True)
+
+    def spread(stored):
+        return jnp.einsum("ju,urc->jrc", pick, stored, preferred_element_type=jnp.float32).astype(narrow)
+
+    arrived = exchange(spread(weights))
+    own_rows = arrived.reshape(own_shape)
+    gathered = lax.all_gather(own_rows, "dp", axis=0, tiled=True)
+    moments = jnp.concatenate([first_moment, second_moment], axis=1).astype(narrow)
+    moments_sent, _ = lax.optimization_barrier((spread(moments), arrived))
+    moments_here = exchange(moments_sent)
+    gathered, moments_here = lax.optimization_barrier((gathered, moments_here))
+    projected = jnp.dot(inputs, gathered, preferred_element_type=jnp.float32)
     grad_proj = silu_grads(projected, hidden_grad[0, 0], live_mask)
-    columns = inputs
-    summed_data = lax.psum_scatter(
-        lax.dot_general(
-            columns, grad_proj, (((0,), (0,)), ((), ())), preferred_element_type=jnp.float32
-        ).astype(jnp.bfloat16),
-        "dp",
-        scatter_dimension=0,
-        tiled=True,
-    ).astype(jnp.float32)
-    at_home = lax.all_to_all(
-        summed_data.reshape(expert_count, span_rows, col_total),
-        "expert",
-        split_axis=0,
-        concat_axis=0,
-        tiled=True,
-    )
-    block_grad = lax.dot_general(
-        owner_table,
-        at_home.reshape(expert_count, span_rows * col_total),
-        (((0,), (0,)), ((), ())),
-        precision=lax.Precision.HIGHEST,
-    )
-    block_grad = block_grad.reshape(block_total, span_rows, col_total)
-    first_sent = jnp.take(first_moment, placement, axis=0)
-    second_sent = jnp.take(second_moment, placement, axis=0)
-    grad_sent = jnp.take(block_grad, placement, axis=0)
-    first_here, second_here, grad_here = (
-        lax.all_to_all(first_sent, "expert", split_axis=0, concat_axis=0, tiled=True),
-        lax.all_to_all(second_sent, "expert", split_axis=0, concat_axis=0, tiled=True),
-        lax.all_to_all(grad_sent, "expert", split_axis=0, concat_axis=0, tiled=True),
-    )
-    own_shape = (expert_count * span_rows, col_total)
+    term = lax.dot_general(
+        inputs, grad_proj, (((0,), (0,)), ((), ())), preferred_element_type=jnp.float32
+    ).astype(narrow)
+    summed_data = lax.psum_scatter(term, "dp", scatter_dimension=0, tiled=True)
+    at_home = exchange(summed_data.reshape(expert_count, span_rows, col_total))
+    block_grad = jnp.einsum("jk,krc->jrc", same, at_home, preferred_element_type=jnp.float32).astype(narrow)
+    grad_here = exchange(block_grad)
     updated, moment_one, moment_two = adam_update(
         own_rows,
-        first_here.reshape(own_shape),
-        second_here.reshape(own_shape),
-        grad_here.reshape(own_shape),
+        moments_here[:, :span_rows].reshape(own_shape).astype(jnp.float32),
+        moments_here[:, span_rows:].reshape(own_shape).astype(jnp.float32),
+        grad_here.reshape(own_shape).astype(jnp.float32),
     )
     return (updated[None], moment_one[None], moment_two[None])
 

time: 297 us -> 234 us (0.79)
  waiting for transfers between devices: 158 us -> 108 us
  blocking collectives: 33.6 us -> 65 us
  starting transfers between devices: 37.1 us -> 11.3 us
  local copies, waits for them, and re-layouts: 30.4 us -> 20.5 us
  other arithmetic: 12.9 us -> 5.46 us
    all_gather x1, waiting for transfers between devices: 43.8 us -> 9.94 us  [on_device(): gathered = lax.all_gather(own_rows, 'dp', axis=0, tiled=True)]
    all_to_all x1 -> x2, blocking collectives: 33.6 us -> 65 us  [exchange(): lax.all_to_all(values, 'expert', split_axis=0, concat_axis=0, tiled=True)]
    all_to_all x4 -> x2, waiting for transfers between devices: 73.8 us -> 46 us  [exchange(): lax.all_to_all(values, 'expert', split_axis=0, concat_axis=0, tiled=True)]
    all_to_all x4 -> x2, starting transfers between devices: 37 us -> 11.2 us  [exchange(): lax.all_to_all(values, 'expert', split_axis=0, concat_axis=0, tiled=True)]
    reduce_scatter x1, waiting for transfers between devices: 40.7 us -> 52.1 us  [on_device(): summed_data = lax.psum_scatter(term, 'dp', scatter_dimension=0, tiled=True)]
    gather x4 -> x0, local copies, waits for them, and re-layouts: 10.1 us -> none  [the longest x1 2.88 us: on_device(): outgoing = jnp.take(weights, placement, axis=0)]
    select_n x4 -> x0, other arithmetic: 5.99 us -> none  [the longest x1 2.63 us: on_device(): second_sent = jnp.take(second_moment, placement, axis=0)]
    select_n x3 -> x0, local copies, waits for them, and re-layouts: 4.48 us -> none  [the longest x1 2.7 us: on_device(): second_sent = jnp.take(second_moment, placement, axis=0)]
  transfers between devices with their start and end apart: 6 -> 4, of which waited for: 5 -> 4; matrix products, arithmetic and copies ran while one was open for 9% -> 4% of each run, Pallas kernels for 0% -> 0%
where the time goes in v1:
time: 234 us; the launch traced here: 233 us
  waiting for transfers between devices  108 us (46%)
  blocking collectives  65 us (28%)
  local copies, waits for them, and re-layouts  20.5 us (9%)
  between operations  14.8 us (6%)
  starting transfers between devices  11.3 us (5%)
  matrix products  8.32 us (4%)
  other arithmetic  5.46 us (2%)
    all_to_all x2, blocking collectives, exchange(): lax.all_to_all(values, 'expert', split_axis=0, concat_axis=0, tiled=True)  65 us
    reduce_scatter x1, waiting for transfers between devices, on_device(): summed_data = lax.psum_scatter(term, 'dp', scatter_dimension=0, tiled=True)  52.1 us
    all_to_all x2, waiting for transfers between devices, exchange(): lax.all_to_all(values, 'expert', split_axis=0, concat_axis=0, tiled=True)  46 us
    all_to_all x2, starting transfers between devices, exchange(): lax.all_to_all(values, 'expert', split_axis=0, concat_axis=0, tiled=True)  11.2 us
    all_gather x1, waiting for transfers between devices, on_device(): gathered = lax.all_gather(own_rows, 'dp', axis=0, tiled=True)  9.94 us
    unnamed x12, local copies, waits for them, and re-layouts  7.01 us
  transfers between devices with their start and end apart: 4, of which 4 were waited for; matrix products, arithmetic and copies ran while one was open for 4% of the time, Pallas kernels for 0%

profile of v1, /device:TPU:16, one launch (start us, length us, event | category | flops | bytes accessed | tf_op | source)
XLA Modules:
  0.0 233.5 jit_solution(11896177370033334054)
XLA Ops:
  7.2 0.0 copy-start
  7.2 0.0 copy-start.4
  7.2 0.0 copy-start.2
  7.2 0.0 copy-start.3
  7.2 0.0 all-gather.2.cloned.1.call-start
  7.3 1.4 convolution_convert_fusion.2
  8.6 0.3 copy.20
  8.9 33.6 %all_to_all.20 = bf16[64,7,512]{2,1,0:T(8,128)(2,1)S(1)} all-to-all(bf16[64,7,512]{2,1,0:T(8,128)(2,1)S(1)} %copy.20), channel_id=1, replica_groups=mesh['dp'=8,'expert'=64] {'expert'}, dimensions={0} | all-to-all | bytes 917504 | tf_op jit(solution)/shard_map/all_to_all | solution.py:55
  42.5 0.9 reshape.142
  43.4 0.0 all-gather.2.cloned.1.call-update
  43.5 0.0 copy-done.2
  43.5 0.0 copy-done.3
  43.5 0.0 copy-done.4
  43.5 0.4 convolution_convert_fusion.1
  44.0 1.5 copy.21
  45.5 4.7 %all-to-all-start.1 = ((bf16[64,14,512]{2,1,0:T(8,128)(2,1)}), bf16[64,14,512]{2,1,0:T(8,128)(2,1)S(1)}, u32[]{:S(2)}, u32[]{:S(2)}) async-start(bf16[64,14,512]{2,1,0:T(8,128)(2,1)} %copy.21), calls=%async_computation.1 | async-start | bytes 2097152 | tf_op jit(solution)/shard_map/all_to_all | solution.py:55
  50.2 0.0 reduce-scatter.4.cloned.1.call-start
  50.2 1.0 copy.22
  51.9 33.5 %all-to-all-done.1 = bf16[64,14,512]{2,1,0:T(8,128)(2,1)S(1)} async-done(((bf16[64,14,512]{2,1,0:T(8,128)(2,1)}), bf16[64,14,512]{2,1,0:T(8,128)(2,1)S(1)}, u32[]{:S(2)}, u32[]{:S(2)}) %all-to-all-start.1) | async-done | bytes 917536 | tf_op jit(solution)/shard_map/all_to_all | solution.py:55
  85.4 9.9 %all-gather.2.cloned.1.call-done = bf16[3584,512]{1,0:T(8,128)(2,1)} async-done(((bf16[448,512]{1,0:T(8,128)(2,1)}), bf16[3584,512]{1,0:T(8,128)(2,1)}) %all-gather.2.cloned.1.call-update) | async-done | bytes 3670032 | tf_op jit(solution)/shard_map/all_gather | solution.py:62
  95.3 0.0 copy-done
  95.3 3.2 %fusion.4 = f32[256,512]{0,1:T(8,128)S(1)} fusion(bf16[3584,512]{1,0:T(8,128)(2,1)} %all-gather.2.cloned.1.call-done, bf16[1,1,256,3584]{3,2,1,0:T(8,128)(2,1)S(1)} %copy-done), kind=kOutput, calls=%fused_computation.9 | convolution fusion | flops 939524096 | bytes 6029312 | tf_op jit(solution)/shard_map/dot_general | solution.py:67
  98.5 0.2 fusion.11
  98.7 3.0 %fusion = bf16[3584,512]{0,1:T(8,128)(2,1)} fusion(bf16[1,1,256,3584]{3,2,1,0:T(8,128)(2,1)S(1)} %copy-done, bf16[256,256]{0,1:T(8,128)(2,1)S(1)} %get-tuple-element.15, bf16[256,256]{0,1:T(8,128)(2,1)S(1)} %get-tuple-element.14), kind=kOutput, calls=%fused_computation.1 | convolution fusion | flops 941883392 | bytes 5767168 | tf_op jit(solution)/shard_map/dot_general | solution.py:69
  101.6 6.0 %copy.26 = bf16[3584,512]{1,0:T(8,128)(2,1)} copy(bf16[3584,512]{0,1:T(8,128)(2,1)} %fusion) | data formatting | bytes 7340032
  107.6 0.0 reduce-scatter.4.cloned.1.call-update
  107.6 52.1 %reduce-scatter.4.cloned.1.call-done = bf16[448,512]{1,0:T(8,128)(2,1)} async-done(((bf16[3584,512]{1,0:T(8,128)(2,1)}), bf16[448,512]{1,0:T(8,128)(2,1)}) %reduce-scatter.4.cloned.1.call-update) | async-done | bytes 458768 | tf_op jit(solution)/shard_map/reduce_scatter | solution.py:72
  159.7 2.0 reshape.143
  161.7 31.4 %all_to_all.21 = bf16[64,7,512]{2,1,0:T(8,128)(2,1)S(1)} all-to-all(bf16[64,7,512]{2,1,0:T(8,128)(2,1)} %reshape.143), channel_id=1, replica_groups=mesh['dp'=8,'expert'=64] {'expert'}, dimensions={0} | all-to-all | bytes 917504 | tf_op jit(solution)/shard_map/all_to_all | solution.py:55
  193.1 0.3 convolution_convert_fusion.3
  193.4 1.1 copy.25
  194.5 6.6 %all-to-all-start.3 = ((bf16[64,7,512]{2,1,0:T(8,128)(2,1)}), bf16[64,7,512]{2,1,0:T(8,128)(2,1)}, u32[]{:S(2)}, u32[]{:S(2)}) async-start(bf16[64,7,512]{2,1,0:T(8,128)(2,1)} %copy.25), calls=%async_computation.3 | async-start | bytes 1048576 | tf_op jit(solution)/shard_map/all_to_all | solution.py:55
  201.0 1.1 reshape.144
  202.1 1.6 convert_multiply_fusion
  203.7 0.0 copy-start.1
  203.7 2.4 %mul.128 = f32[1,448,512]{2,1,0:T(8,128)} reshape(f32[64,7,512]{2,1,0:T(8,128)} %get-tuple-element.13) | data formatting | bytes 1835008 | tf_op jit(solution)/shard_map/mul | solution.py:29
  206.1 2.3 mul.138
  208.4 12.5 %all-to-all-done.3 = bf16[64,7,512]{2,1,0:T(8,128)(2,1)} async-done(((bf16[64,7,512]{2,1,0:T(8,128)(2,1)}), bf16[64,7,512]{2,1,0:T(8,128)(2,1)}, u32[]{:S(2)}, u32[]{:S(2)}) %all-to-all-start.3) | async-done | bytes 458784 | tf_op jit(solution)/shard_map/all_to_all | solution.py:55
  220.9 2.1 reshape.146
  223.0 0.0 copy-done.1
  223.0 3.6 %subtract_convert_fusion = (bf16[1,448,512]{2,1,0:T(8,128)(2,1)}, f32[1,448,512]{2,1,0:T(8,128)}, f32[1,448,512]{2,1,0:T(8,128)}) fusion(f32[1,448,512]{2,1,0:T(8,128)S(1)} %copy-done.1, f32[1,448,512]{2,1,0:T(8,128)} %mul.128, f32[1,448,512]{2,1,0:T(8,128)} %reshape.146, f32[1,448,512]{2,1,0:T(8,128)} %mul.138), kind=kLoop, calls=%fused_computation.13 | loop fusion | flops 3211264 | bytes 5963776 | tf_op jit(solution)/shard_map/convert_element_type | solution.py:38
  (3 shorter events, 0.0 us)
Async XLA Ops:
  7.2 88.2 %copy-start = (bf16[1,1,256,3584]{3,2,1,0:T(8,128)(2,1)S(1)}, bf16[1,1,256,3584]{3,2,1,0:T(8,128)(2,1)}, u32[]{:S(2)}) copy-start(bf16[1,1,256,3584]{3,2,1,0:T(8,128)(2,1)} %param.12) | copy-start | bytes 5505028
  7.2 36.4 %copy-start.4 = (s32[64]{0:T(128)S(1)}, s32[64]{0:T(128)}, u32[]{:S(2)}) copy-start(s32[64]{0:T(128)} %param.10) | copy-start | bytes 772
  7.2 36.3 %copy-start.2 = (f32[16,7,512]{2,0,1:T(8,128)S(1)}, f32[16,7,512]{2,0,1:T(8,128)}, u32[]{:S(2)}) copy-start(f32[16,7,512]{2,0,1:T(8,128)} %param.8) | copy-start | bytes 688132
  7.2 36.3 %copy-start.3 = (f32[16,7,512]{2,0,1:T(8,128)S(1)}, f32[16,7,512]{2,0,1:T(8,128)}, u32[]{:S(2)}) copy-start(f32[16,7,512]{2,0,1:T(8,128)} %param.9) | copy-start | bytes 688132
  7.2 88.1 %all-gather.2.cloned.1.call-start = ((), (), s32[]{:S(2)}) async-start(), calls=%async_computation.5 | async-start | bytes 4128768 | tf_op jit(solution)/shard_map/all_gather | solution.py:62
  45.5 39.9 %all-to-all-start.1 = ((bf16[64,14,512]{2,1,0:T(8,128)(2,1)}), bf16[64,14,512]{2,1,0:T(8,128)(2,1)S(1)}, u32[]{:S(2)}, u32[]{:S(2)}) async-start(bf16[64,14,512]{2,1,0:T(8,128)(2,1)} %copy.21), calls=%async_computation.1 | async-start | bytes 2097152 | tf_op jit(solution)/shard_map/all_to_all | solution.py:55
  50.2 109.5 %reduce-scatter.4.cloned.1.call-start = ((), (), s32[]{:S(2)}) async-start(), calls=%async_computation.6 | async-start | bytes 4128768 | tf_op jit(solution)/shard_map/reduce_scatter | solution.py:72
  194.5 26.5 %all-to-all-start.3 = ((bf16[64,7,512]{2,1,0:T(8,128)(2,1)}), bf16[64,7,512]{2,1,0:T(8,128)(2,1)}, u32[]{:S(2)}, u32[]{:S(2)}) async-start(bf16[64,7,512]{2,1,0:T(8,128)(2,1)} %copy.25), calls=%async_computation.3 | async-start | bytes 1048576 | tf_op jit(solution)/shard_map/all_to_all | solution.py:55
  203.7 19.3 %copy-start.1 = (f32[1,448,512]{2,1,0:T(8,128)S(1)}, f32[1,448,512]{2,1,0:T(8,128)}, u32[]{:S(2)}) copy-start(f32[1,448,512]{2,1,0:T(8,128)} %reshape.144) | copy-start | bytes 2752516
Sparse Core Ops, SparseCore 0:
  43.6 51.6 all-gather.1
  107.8 51.8 reduce-scatter.3
